TPU v7x, 32 devices: a whole 2x2x4 slice. The times are simulated.
32 devices in a mesh: inst: 4 (over x, core), gx: 2 (over y), gy: 4 (over z).
Axes of the slice: x: 2, y: 2, z: 4, core: 2. Of those that a mesh axis runs over, the one named last changes fastest.
Arguments:
- state: float32 [8, 5, 16, 32, 128], P('inst', None, 'gx', 'gy'), may hold values from -6 to 6
- source: float32 [8, 5, 16, 32, 128], P('inst', None, 'gx', 'gy'), may hold values from -60 to 60
- jacobian: float32 [8, 5, 5, 16, 32, 128], P('inst', None, None, 'gx', 'gy'), may hold values from -1.5 to 16, as said below
- couplings: float32 [6, 5, 5], replicated, may hold values from -0.625 to 0.625
- omega: float32 [1], replicated, may hold values from 0.2 to 0.6
Outputs:
- state_next: float32 [8, 5, 16, 32, 128], P('inst', None, 'gx', 'gy')
- last_residual: float32 [8, 5, 16, 32, 128], P('inst', None, 'gx', 'gy')
Inputs may be any that keep to these rules, and one draw needn't show every extreme that they name: In every block jacobian[n, :, :, cell] each diagonal entry lies in 8 to 16 and exceeds the sum of magnitudes of the other entries of its row by 2 or more.
All inputs are finite; a program needn't handle non-finite values.
Results may differ from a plain program's by a relative error of at most 0.0003.
Values sent between devices are 32-bit elements; how exact they have to be, the bound alone decides.
A program may use at most 64 MiB of HBM per device.

v0:
```python
import functools
import math

import jax
import jax.numpy as jnp
from jax import lax
from jax.experimental import pallas as pl
from jax.experimental.pallas import tpu as pltpu
from jax.sharding import PartitionSpec as P

ITERS = 3
LAG = 2
MESH = pl.DeviceIdType.MESH


def derivative(offset, total):
    offset = offset % total
    if offset > total // 2:
        offset -= total
    if offset == 0:
        return 0.0
    angle = math.pi * offset / total
    return 0.5 * (-1.0) ** offset * math.cos(angle) / math.sin(angle)


def factor(blocks):
    size = len(blocks)
    matrix = [list(row) for row in blocks]
    for pivot in range(size):
        matrix[pivot][pivot] = 1.0 / matrix[pivot][pivot]
        for target in range(pivot + 1, size):
            ratio = matrix[target][pivot] * matrix[pivot][pivot]
            matrix[target][pivot] = ratio
            for column in range(pivot + 1, size):
                matrix[target][column] = matrix[target][column] - ratio * matrix[pivot][column]
    return matrix


def substitute(matrix, right):
    size = len(right)
    vector = list(right)
    for pivot in range(size):
        for target in range(pivot + 1, size):
            vector[target] = vector[target] - matrix(target, pivot) * vector[pivot]
    result = [None] * size
    for pivot in reversed(range(size)):
        total = vector[pivot]
        for column in range(pivot + 1, size):
            total = total - matrix(pivot, column) * result[column]
        result[pivot] = total * matrix(pivot, pivot)
    return result


def weighted(weights, pieces):
    total = None
    for weight, piece in zip(weights, pieces):
        if isinstance(weight, float) and weight == 0.0:
            continue
        term = weight * piece
        total = term if total is None else total + term
    return total


def kernel(
    ranks, count_x, count_y,
    state, source, jacobian, couplings, omega,
    state_next, last_residual,
    cur, peer, part, got, relayed, edge_out, edge_in,
    rhs, blocks, lu, weights_in, speed_in,
    load_sem, x_send, core_send, edge_send, side_send,
    first_recv, peer_recv, relay_recv, got_recv, edge_recv, side_recv,
):
    local, nvar, planes, rows, depth = state.shape
    total = local * ranks
    pairs = ranks // 2
    rank = lax.axis_index("inst")
    at_x = lax.axis_index("gx")
    at_y = lax.axis_index("gy")
    pair = rank // 2
    core = rank % 2
    partner = pair * 2 + 1 - core
    up = (at_y + 1) % count_y
    down = (at_y + count_y - 1) % count_y
    has_low = at_x > 0
    has_high = at_x < count_x - 1
    flip = at_x % 2 == 0
    hops = range(1, pairs)

    def plane_of(step):
        return jnp.where(flip, planes - 1 - step, step)

    def load_state(x):
        return pltpu.make_async_copy(state.at[:, :, x], cur.at[0, x + 1], load_sem.at[0])

    loads = [
        pltpu.make_async_copy(jacobian, blocks, load_sem.at[1]),
        pltpu.make_async_copy(source, rhs, load_sem.at[2]),
        pltpu.make_async_copy(couplings, weights_in, load_sem.at[3]),
        pltpu.make_async_copy(omega, speed_in, load_sem.at[4]),
    ]

    def remote(source_ref, target_ref, send, recv, **where):
        return pltpu.make_async_remote_copy(
            source_ref, target_ref, send, recv, device_id=where, device_id_type=MESH)

    def to_peer(k, x):
        recv = first_recv.at[0] if k == 0 else peer_recv.at[k - 1, x]
        return remote(cur.at[k, x + 1], peer.at[k, x], core_send.at[0], recv, inst=partner)

    def to_pair(k, x, hop):
        target = ((pair + hop) % pairs) * 2 + core
        outgoing = cur.at[0, x + 1] if k == 0 else part.at[k - 1, hop - 1, x]
        return remote(
            outgoing, got.at[k, hop - 1, x], x_send.at[0], got_recv.at[k % 2, hop - 1, x],
            inst=target)

    def relay(x, hop):
        return remote(
            got.at[0, hop - 1, x], relayed.at[hop - 1, x], core_send.at[1],
            relay_recv.at[hop - 1, x], inst=partner)

    def to_side(k, x, side):
        return remote(
            edge_out.at[k, x, side], edge_in.at[k, x, side], edge_send.at[0],
            edge_recv.at[k % 2, x], gy=up if side == 0 else down)

    def both_sides(k, x):
        return remote(
            edge_out.at[k, x], edge_in.at[k, x], edge_send.at[0], edge_recv.at[k % 2, x], gy=up)

    def to_next(k):
        return remote(
            cur.at[k, planes], cur.at[k, 0], side_send.at[0], side_recv.at[0, k], gx=at_x + 1)

    def to_last(k):
        return remote(
            cur.at[k, 1], cur.at[k, planes + 1], side_send.at[1], side_recv.at[1, k],
            gx=at_x - 1)

    def send_planes(k, x):
        to_peer(k, x).start()

        @pl.when(jnp.logical_and(x == planes - 1, has_high))
        def _():
            to_next(k).start()

        @pl.when(jnp.logical_and(x == 0, has_low))
        def _():
            to_last(k).start()

    def send_edges(k, x, field):
        for n in range(local):
            for v in range(nvar):
                at = n * nvar + v
                edge_out[k, x, 1, at:at + 1] = field[n][v][:1]
                edge_out[k, x, 0, at:at + 1] = field[n][v][rows - 1:]

    def start_edges(k, x):
        to_side(k, x, 0).start()
        to_side(k, x, 1).start()

    def mine(k, x):
        return [[cur[k, x + 1, n, v] for v in range(nvar)] for n in range(local)]

    even = core == 0

    def weights_of(hop, a):
        own = [derivative(2 * local * hop + a - b, total) for b in range(local)]
        other = [
            jnp.where(
                even,
                jnp.float32(derivative(2 * local * hop - local + a - b, total)),
                jnp.float32(derivative(2 * local * hop + local + a - b, total)),
            )
            for b in range(local)
        ]
        return own + other

    def send_parts(k, x):
        to_peer(k, x).wait_recv()
        for hop in hops:
            for a in range(local):
                weights = weights_of(hop, a)
                for v in range(nvar):
                    pieces = [cur[k, x + 1, b, v] for b in range(local)]
                    pieces += [peer[k, x, b, v] for b in range(local)]
                    part[k - 1, hop - 1, x, a, v] = weighted(weights, pieces)
            to_pair(k, x, hop).start()

    for step in range(planes):
        load_state(plane_of(step)).start()
    for copy in loads:
        copy.start()

    barrier = pltpu.get_barrier_semaphore()

    def greet(**where):
        pl.semaphore_signal(barrier, inc=1, device_id=where, device_id_type=MESH)

    greet(inst=partner)
    for hop in hops:
        greet(inst=((pair + hop) % pairs) * 2 + core)
    greet(gy=up)
    greet(gy=down)

    @pl.when(has_low)
    def _():
        greet(gx=at_x - 1)

    @pl.when(has_high)
    def _():
        greet(gx=at_x + 1)

    zero = jnp.zeros((local, nvar, rows, depth), jnp.float32)

    @pl.when(jnp.logical_not(has_low))
    def _():
        for k in range(ITERS):
            cur[k, 0] = zero

    @pl.when(jnp.logical_not(has_high))
    def _():
        for k in range(ITERS):
            cur[k, planes + 1] = zero

    sides = has_low.astype(jnp.int32) + has_high.astype(jnp.int32)
    held = cur.at[0, 1:planes + 1]
    pltpu.make_async_copy(held, held, load_sem.at[0]).wait()
    pl.semaphore_wait(barrier, pairs + 2 + sides)

    @pl.loop(0, planes)
    def _(step):
        x = plane_of(step)
        for hop in hops:
            to_pair(0, x, hop).start()

    @pl.loop(0, planes)
    def _(step):
        x = plane_of(step)
        send_edges(0, x, mine(0, x))
        send_planes(0, x)
        start_edges(0, x)

    for copy in loads:
        copy.wait()

    @pl.loop(0, planes)
    def _(step):
        x = plane_of(step)
        for n in range(local):
            matrix = factor([[blocks[n, v, w, x] for w in range(nvar)] for v in range(nvar)])
            for v in range(nvar):
                for w in range(nvar):
                    lu[n, v, w, x] = matrix[v][w]

    row_at = lax.broadcasted_iota(jnp.int32, (rows, depth), 0)
    lane_at = lax.broadcasted_iota(jnp.int32, (rows, depth), 1)
    first_row, final_row = row_at == 0, row_at == rows - 1
    first_lane, final_lane = lane_at == 0, lane_at == depth - 1
    speed = speed_in[0]
    lag = min(LAG, planes)

    def near_side(k, x):
        result = [[None] * nvar for _ in range(local)]
        for w in range(nvar):
            for n in range(local):
                field = cur[k, x + 1, n, w]
                at = n * nvar + w
                shifted = [
                    cur[k, x, n, w],
                    cur[k, x + 2, n, w],
                    jnp.where(first_row, edge_in[k, x, 0, at:at + 1], pltpu.roll(field, 1, 0)),
                    jnp.where(
                        final_row, edge_in[k, x, 1, at:at + 1], pltpu.roll(field, rows - 1, 0)),
                    jnp.where(first_lane, 0.0, pltpu.roll(field, 1, 1)),
                    jnp.where(final_lane, 0.0, pltpu.roll(field, depth - 1, 1)),
                ]
                for v in range(nvar):
                    term = weighted([weights_in[v, d, w] for d in range(6)], shifted)
                    last = result[n][v]
                    result[n][v] = term if last is None else last + term
        for n in range(local):
            weights = weights_of(0, n)
            for v in range(nvar):
                pieces = [cur[k, x + 1, b, v] for b in range(local)]
                pieces += [peer[k, x, b, v] for b in range(local)]
                spectral = weighted(weights, pieces)
                result[n][v] = rhs[n, v, x] - result[n][v] - speed * spectral
        return result

    def far_side(k, x, n, v):
        spectral = None
        for hop in hops:
            if k == 0:
                pieces = [got[k, hop - 1, x, b, v] for b in range(local)]
                pieces += [relayed[hop - 1, x, b, v] for b in range(local)]
                term = weighted(weights_of(hop, n), pieces)
            else:
                term = got[k, hop - 1, x, n, v]
            spectral = term if spectral is None else spectral + term
        return spectral

    def pass_on(x):
        for hop in hops:
            to_pair(0, x, hop).wait_recv()
            relay(x, hop).start()

    pass_on(plane_of(0))
    pltpu.make_async_copy(peer.at[0], peer.at[0], first_recv.at[0]).wait()

    for k in range(ITERS):
        final_pass = k == ITERS - 1

        @pl.loop(0, planes)
        def _(step, k=k, final_pass=final_pass):
            x = plane_of(step)

            @pl.when(jnp.logical_and(x == 0, has_low))
            def _():
                to_next(k).wait_recv()

            @pl.when(jnp.logical_and(x == planes - 1, has_high))
            def _():
                to_last(k).wait_recv()

            both_sides(k, x).wait_recv()
            rights = near_side(k, x)
            if final_pass:
                own = mine(k, x)
                for n in range(local):
                    for v in range(nvar):
                        for w in range(nvar):
                            rights[n][v] = rights[n][v] - blocks[n, v, w, x] * own[n][w]
            if k == 0:

                @pl.when(step + 1 < planes)
                def _():
                    pass_on(plane_of(step + 1))

                for hop in hops:
                    relay(x, hop).wait_recv()
            else:
                for hop in hops:
                    to_pair(k, x, hop).wait_recv()
            fields = []
            for n in range(local):
                right = rights[n]
                if pairs > 1:
                    right = [right[v] - speed * far_side(k, x, n, v) for v in range(nvar)]
                answer = substitute(lambda v, w: lu[n, v, w, x], right)
                for v in range(nvar):
                    if final_pass:
                        last_residual[n, v, x] = right[v]
                        state_next[n, v, x] = own[n][v] + answer[v]
                    else:
                        cur[k + 1, x + 1, n, v] = answer[v]
                fields.append(answer)
            if not final_pass:
                send_edges(k + 1, x, fields)
                send_planes(k + 1, x)
                start_edges(k + 1, x)

                @pl.when(step >= lag)
                def _():
                    send_parts(k + 1, plane_of(step - lag))

            if k > 0:

                @pl.when(step < lag)
                def _():
                    send_parts(k, plane_of(planes - lag + step))

    for hop in hops:
        sent = got.at[:, hop - 1]
        remote(sent, sent, x_send.at[0], x_send.at[0], inst=partner).wait_send()
    remote(peer, peer, core_send.at[0], core_send.at[0], inst=partner).wait_send()
    remote(relayed, relayed, core_send.at[1], core_send.at[1], inst=partner).wait_send()
    remote(edge_out, edge_out, edge_send.at[0], edge_send.at[0], inst=partner).wait_send()
    layer = cur.at[:, 0]

    @pl.when(has_high)
    def _():
        remote(layer, layer, side_send.at[0], side_send.at[0], inst=partner).wait_send()

    @pl.when(has_low)
    def _():
        remote(layer, layer, side_send.at[1], side_send.at[1], inst=partner).wait_send()


def store(field, residual, state_next, last_residual, sems):
    copies = [
        pltpu.make_async_copy(field, state_next, sems.at[0]),
        pltpu.make_async_copy(residual, last_residual, sems.at[1]),
    ]
    for copy in copies:
        copy.start()
    for copy in copies:
        copy.wait()


def solution(mesh):
    ranks, count_x, count_y = mesh.shape["inst"], mesh.shape["gx"], mesh.shape["gy"]

    def shards(state, source, jacobian, couplings, omega):
        local, nvar, planes, rows, depth = state.shape
        pairs = ranks // 2
        cell = (local, nvar, rows, depth)
        edge = pltpu.VMEM((ITERS, planes, 2, local * nvar, depth), jnp.float32)
        hbm = pl.BlockSpec(memory_space=pltpu.HBM)
        near = pl.BlockSpec(memory_space=pltpu.VMEM)
        dma = pltpu.SemaphoreType.DMA
        vmem = lambda *lead: pltpu.VMEM(lead + cell, jnp.float32)
        matrices = pltpu.VMEM(jacobian.shape, jnp.float32)
        flows = couplings.transpose(1, 0, 2)
        field, residual = pl.pallas_call(
            functools.partial(kernel, ranks, count_x, count_y),
            out_shape=[pltpu.VMEM(state.shape, jnp.float32)] * 2,
            in_specs=[hbm] * 5,
            out_specs=[near, near],
            scratch_shapes=[
                vmem(ITERS, planes + 2), vmem(ITERS, planes),
                vmem(ITERS - 1, pairs - 1, planes), vmem(ITERS, pairs - 1, planes),
                vmem(pairs - 1, planes), edge, edge,
                pltpu.VMEM(state.shape, jnp.float32), matrices, matrices,
                pltpu.SMEM(flows.shape, jnp.float32), pltpu.SMEM(omega.shape, jnp.float32),
                dma((5,)), dma((1,)), dma((2,)), dma((1,)), dma((2,)),
                dma((1,)), dma((ITERS - 1, planes)), dma((pairs - 1, planes)),
                dma((2, pairs - 1, planes)), dma((2, planes)), dma((2, ITERS)),
            ],
            compiler_params=pltpu.CompilerParams(
                collective_id=0, has_side_effects=True, vmem_limit_bytes=60 * 1024 * 1024),
            name="smooth",
        )(state, source, jacobian, flows, omega)
        return tuple(pl.pallas_call(
            store,
            out_shape=[jax.ShapeDtypeStruct(state.shape, jnp.float32)] * 2,
            in_specs=[near, near],
            out_specs=[hbm, hbm],
            scratch_shapes=[dma((2,))],
            compiler_params=pltpu.CompilerParams(vmem_limit_bytes=16 * 1024 * 1024),
            name="store",
        )(field, residual))

    split = P("inst", None, "gx", "gy", None)
    return jax.shard_map(
        shards,
        mesh=mesh,
        in_specs=(split, split, P("inst", None, None, "gx", "gy", None), P(), P()),
        out_specs=(split, split),
        check_vma=False,
    )
```

profile of v0, /device:TPU:0, one launch (start us, length us, event | category | flops | bytes accessed | tf_op | source)
XLA Modules:
  0.0 31.0 jit_solution(3385785365987175772)
XLA Ops:
  1.3 28.8 %smooth.1 = (f32[2,5,8,8,128]{4,3,2,1,0:T(8,128)S(1)}, f32[2,5,8,8,128]{4,3,2,1,0:T(8,128)S(1)}) custom-call(f32[2,5,8,8,128]{4,3,2,1,0:T(8,128)} %state.1, f32[2,5,8,8,128]{4,3,2,1,0:T(8,128)} %source.1, f32[2,5,5,8,8,128]{5,4,3,2,1,0:T(8,128)} %jacobian.1, f32[5,6,5]{2,1,0:T(8,128)} %bitcast.1, f32[1]{0:T(128)S(6)} %copy.7.omega), custom_call_target="tpu_custom_call" | custom-call | tf_op jit(solution)/shard_map/smooth/pallas_call | solution.py:415
  30.1 0.9 %store.1 = (f32[2,5,8,8,128]{4,3,2,1,0:T(8,128)}, f32[2,5,8,8,128]{4,3,2,1,0:T(8,128)}) custom-call(f32[2,5,8,8,128]{4,3,2,1,0:T(8,128)S(1)} %get-tuple-element.4.field, f32[2,5,8,8,128]{4,3,2,1,0:T(8,128)S(1)} %get-tuple-element.5.residual), custom_call_target="tpu_custom_call" | custom-call | tf_op jit(solution)/shard_map/store/pallas_call | solution.py:434
where the time goes:
time: 31.1 us; the launch traced here: 31 us
  Pallas kernels  29.7 us (95%)
  between operations  1.29 us (4%)
    pallas_call x1, Pallas kernels, shards(): pl.pallas_call(functools.partial(kernel, ranks, count_x, count_y), out_sh...  28.8 us
    pallas_call x1, Pallas kernels, shards(): pl.pallas_call(store, out_shape=[jax.ShapeDtypeStruct(state.shape, jnp.fl...  0.85 us

commit v1 on v0

--- a/solution.py
+++ b/solution.py
@@ -68,7 +68,7 @@
     cur, peer, part, got, relayed, edge_out, edge_in,
     rhs, blocks, lu, weights_in, speed_in,
     load_sem, x_send, core_send, edge_send, side_send,
-    first_recv, peer_recv, relay_recv, got_recv, edge_recv, side_recv,
+    first_recv, peer_recv, relay_recv, got_recv, edge_recv, side_recv, ready,
 ):
     local, nvar, planes, rows, depth = state.shape
     total = local * ranks
@@ -197,19 +197,26 @@
     def greet(**where):
         pl.semaphore_signal(barrier, inc=1, device_id=where, device_id_type=MESH)
 
-    greet(inst=partner)
+    leads = core == 1
+    lead = pair * 2 + 1
+    tail = pair * 2
+
+    @pl.when(jnp.logical_not(leads))
+    def _():
+        greet(inst=lead)
+
     for hop in hops:
-        greet(inst=((pair + hop) % pairs) * 2 + core)
-    greet(gy=up)
-    greet(gy=down)
+        greet(inst=((pair + hop) % pairs) * 2 + 1)
+    greet(inst=tail, gy=up)
+    greet(inst=tail, gy=down)
 
     @pl.when(has_low)
     def _():
-        greet(gx=at_x - 1)
+        greet(inst=tail, gx=at_x - 1)
 
     @pl.when(has_high)
     def _():
-        greet(gx=at_x + 1)
+        greet(inst=tail, gx=at_x + 1)
 
     zero = jnp.zeros((local, nvar, rows, depth), jnp.float32)
 
@@ -226,13 +233,34 @@
     sides = has_low.astype(jnp.int32) + has_high.astype(jnp.int32)
     held = cur.at[0, 1:planes + 1]
     pltpu.make_async_copy(held, held, load_sem.at[0]).wait()
-    pl.semaphore_wait(barrier, pairs + 2 + sides)
+
+    def tell_partner():
+        pl.semaphore_signal(
+            ready.at[0], inc=1, device_id={"inst": partner}, device_id_type=MESH)
+
+    @pl.when(leads)
+    def _():
+        pl.semaphore_wait(barrier, 2 * pairs - 1)
+        tell_partner()
+
+    @pl.when(jnp.logical_not(leads))
+    def _():
+        pl.semaphore_wait(ready.at[0], 1)
 
     @pl.loop(0, planes)
     def _(step):
         x = plane_of(step)
         for hop in hops:
             to_pair(0, x, hop).start()
+
+    @pl.when(leads)
+    def _():
+        pl.semaphore_wait(ready.at[0], 1)
+
+    @pl.when(jnp.logical_not(leads))
+    def _():
+        pl.semaphore_wait(barrier, 4 + 2 * sides)
+        tell_partner()
 
     @pl.loop(0, planes)
     def _(step):
@@ -426,6 +454,7 @@
                 dma((5,)), dma((1,)), dma((2,)), dma((1,)), dma((2,)),
                 dma((1,)), dma((ITERS - 1, planes)), dma((pairs - 1, planes)),
                 dma((2, pairs - 1, planes)), dma((2, planes)), dma((2, ITERS)),
+                pltpu.SemaphoreType.REGULAR((1,)),
             ],
             compiler_params=pltpu.CompilerParams(
                 collective_id=0, has_side_effects=True, vmem_limit_bytes=60 * 1024 * 1024),

time: 31.1 us -> 30 us (0.965)
  Pallas kernels: 29.7 us -> 28.6 us
    pallas_call x1, Pallas kernels: 28.8 us -> 27.7 us  [shards(): pl.pallas_call(functools.partial(kernel, ranks, count_x, count_y), out_sh...]
where the time goes in v1:
time: 30 us; the launch traced here: 29.8 us
  Pallas kernels  28.6 us (95%)
  between operations  1.29 us (4%)
    pallas_call x1, Pallas kernels, shards(): pl.pallas_call(functools.partial(kernel, ranks, count_x, count_y), out_sh...  27.7 us
    pallas_call x1, Pallas kernels, shards(): pl.pallas_call(store, out_shape=[jax.ShapeDtypeStruct(state.shape, jnp.fl...  0.85 us

profile of v1, /device:TPU:0, one launch (start us, length us, event | category | flops | bytes accessed | tf_op | source)
XLA Modules:
  0.0 29.8 jit_solution(16579474379464525003)
XLA Ops:
  1.3 27.7 %smooth.1 = (f32[2,5,8,8,128]{4,3,2,1,0:T(8,128)S(1)}, f32[2,5,8,8,128]{4,3,2,1,0:T(8,128)S(1)}) custom-call(f32[2,5,8,8,128]{4,3,2,1,0:T(8,128)} %state.1, f32[2,5,8,8,128]{4,3,2,1,0:T(8,128)} %source.1, f32[2,5,5,8,8,128]{5,4,3,2,1,0:T(8,128)} %jacobian.1, f32[5,6,5]{2,1,0:T(8,128)} %bitcast.1, f32[1]{0:T(128)S(6)} %copy.7.omega), custom_call_target="tpu_custom_call" | custom-call | tf_op jit(solution)/shard_map/smooth/pallas_call | solution.py:443
  29.0 0.9 %store.1 = (f32[2,5,8,8,128]{4,3,2,1,0:T(8,128)}, f32[2,5,8,8,128]{4,3,2,1,0:T(8,128)}) custom-call(f32[2,5,8,8,128]{4,3,2,1,0:T(8,128)S(1)} %get-tuple-element.4.field, f32[2,5,8,8,128]{4,3,2,1,0:T(8,128)S(1)} %get-tuple-element.5.residual), custom_call_target="tpu_custom_call" | custom-call | tf_op jit(solution)/shard_map/store/pallas_call | solution.py:463

commit v2 on v1

--- a/solution.py
+++ b/solution.py
@@ -9,7 +9,8 @@
 from jax.sharding import PartitionSpec as P
 
 ITERS = 3
-LAG = 2
+LAG = 1
+GROUP = 2
 MESH = pl.DeviceIdType.MESH
 
 
@@ -65,10 +66,10 @@
     ranks, count_x, count_y,
     state, source, jacobian, couplings, omega,
     state_next, last_residual,
-    cur, peer, part, got, relayed, edge_out, edge_in,
-    rhs, blocks, lu, weights_in, speed_in,
+    cur, peer, part, got, edge_out, edge_in,
+    cells, lu, weights_in, speed_in,
     load_sem, x_send, core_send, edge_send, side_send,
-    first_recv, peer_recv, relay_recv, got_recv, edge_recv, side_recv, ready,
+    first_recv, peer_recv, got_recv, edge_recv, side_recv, ready,
 ):
     local, nvar, planes, rows, depth = state.shape
     total = local * ranks
@@ -85,6 +86,7 @@
     has_high = at_x < count_x - 1
     flip = at_x % 2 == 0
     hops = range(1, pairs)
+    group = GROUP if planes % GROUP == 0 else 1
 
     def plane_of(step):
         return jnp.where(flip, planes - 1 - step, step)
@@ -93,10 +95,10 @@
         return pltpu.make_async_copy(state.at[:, :, x], cur.at[0, x + 1], load_sem.at[0])
 
     loads = [
-        pltpu.make_async_copy(jacobian, blocks, load_sem.at[1]),
-        pltpu.make_async_copy(source, rhs, load_sem.at[2]),
-        pltpu.make_async_copy(couplings, weights_in, load_sem.at[3]),
-        pltpu.make_async_copy(omega, speed_in, load_sem.at[4]),
+        pltpu.make_async_copy(jacobian, cells.at[:, :, :nvar], load_sem.at[1]),
+        pltpu.make_async_copy(source, cells.at[:, :, nvar], load_sem.at[1]),
+        pltpu.make_async_copy(couplings, weights_in, load_sem.at[2]),
+        pltpu.make_async_copy(omega, speed_in, load_sem.at[3]),
     ]
 
     def remote(source_ref, target_ref, send, recv, **where):
@@ -116,25 +118,25 @@
 
     def relay(x, hop):
         return remote(
-            got.at[0, hop - 1, x], relayed.at[hop - 1, x], core_send.at[1],
-            relay_recv.at[hop - 1, x], inst=partner)
+            got.at[0, hop - 1, x], peer.at[ITERS + hop - 1, x], core_send.at[0],
+            peer_recv.at[1 if hop == 1 else ITERS + hop - 3, x], inst=partner)
 
     def to_side(k, x, side):
         return remote(
             edge_out.at[k, x, side], edge_in.at[k, x, side], edge_send.at[0],
-            edge_recv.at[k % 2, x], gy=up if side == 0 else down)
+            edge_recv.at[k % 2, x // group], gy=up if side == 0 else down)
 
     def both_sides(k, x):
-        return remote(
-            edge_out.at[k, x], edge_in.at[k, x], edge_send.at[0], edge_recv.at[k % 2, x], gy=up)
+        some = edge_in.at[k, :group]
+        return remote(some, some, edge_send.at[0], edge_recv.at[k % 2, x // group], gy=up)
 
     def to_next(k):
         return remote(
-            cur.at[k, planes], cur.at[k, 0], side_send.at[0], side_recv.at[0, k], gx=at_x + 1)
+            cur.at[k, planes], cur.at[k, 0], side_send.at[0], side_recv.at[0, k % 2], gx=at_x + 1)
 
     def to_last(k):
         return remote(
-            cur.at[k, 1], cur.at[k, planes + 1], side_send.at[1], side_recv.at[1, k],
+            cur.at[k, 1], cur.at[k, planes + 1], side_send.at[1], side_recv.at[1, k % 2],
             gx=at_x - 1)
 
     def send_planes(k, x):
@@ -187,37 +189,37 @@
                     part[k - 1, hop - 1, x, a, v] = weighted(weights, pieces)
             to_pair(k, x, hop).start()
 
+    barrier = pltpu.get_barrier_semaphore()
+
+    def greet(**where):
+        pl.semaphore_signal(barrier, inc=1, device_id=where, device_id_type=MESH)
+
+    leads = core == 1
+    lead = pair * 2 + 1
+    tail = pair * 2
+
+    @pl.when(jnp.logical_not(leads))
+    def _():
+        greet(inst=lead)
+
+    for hop in hops:
+        greet(inst=((pair + hop) % pairs) * 2 + 1)
+    greet(inst=tail, gy=up)
+    greet(inst=tail, gy=down)
+
+    @pl.when(has_low)
+    def _():
+        greet(inst=lead, gx=at_x - 1)
+
+    @pl.when(has_high)
+    def _():
+        greet(inst=lead, gx=at_x + 1)
+
     for step in range(planes):
         load_state(plane_of(step)).start()
     for copy in loads:
         copy.start()
 
-    barrier = pltpu.get_barrier_semaphore()
-
-    def greet(**where):
-        pl.semaphore_signal(barrier, inc=1, device_id=where, device_id_type=MESH)
-
-    leads = core == 1
-    lead = pair * 2 + 1
-    tail = pair * 2
-
-    @pl.when(jnp.logical_not(leads))
-    def _():
-        greet(inst=lead)
-
-    for hop in hops:
-        greet(inst=((pair + hop) % pairs) * 2 + 1)
-    greet(inst=tail, gy=up)
-    greet(inst=tail, gy=down)
-
-    @pl.when(has_low)
-    def _():
-        greet(inst=tail, gx=at_x - 1)
-
-    @pl.when(has_high)
-    def _():
-        greet(inst=tail, gx=at_x + 1)
-
     zero = jnp.zeros((local, nvar, rows, depth), jnp.float32)
 
     @pl.when(jnp.logical_not(has_low))
@@ -240,7 +242,7 @@
 
     @pl.when(leads)
     def _():
-        pl.semaphore_wait(barrier, 2 * pairs - 1)
+        pl.semaphore_wait(barrier, 2 * pairs - 1 + 2 * sides)
         tell_partner()
 
     @pl.when(jnp.logical_not(leads))
@@ -252,6 +254,7 @@
         x = plane_of(step)
         for hop in hops:
             to_pair(0, x, hop).start()
+        send_planes(0, x)
 
     @pl.when(leads)
     def _():
@@ -259,24 +262,24 @@
 
     @pl.when(jnp.logical_not(leads))
     def _():
-        pl.semaphore_wait(barrier, 4 + 2 * sides)
+        pl.semaphore_wait(barrier, 4)
         tell_partner()
 
     @pl.loop(0, planes)
     def _(step):
         x = plane_of(step)
         send_edges(0, x, mine(0, x))
-        send_planes(0, x)
         start_edges(0, x)
 
-    for copy in loads:
+    pltpu.make_async_copy(cells, cells, load_sem.at[1]).wait()
+    for copy in loads[2:]:
         copy.wait()
 
     @pl.loop(0, planes)
     def _(step):
         x = plane_of(step)
         for n in range(local):
-            matrix = factor([[blocks[n, v, w, x] for w in range(nvar)] for v in range(nvar)])
+            matrix = factor([[cells[n, v, w, x] for w in range(nvar)] for v in range(nvar)])
             for v in range(nvar):
                 for w in range(nvar):
                     lu[n, v, w, x] = matrix[v][w]
@@ -313,7 +316,7 @@
                 pieces = [cur[k, x + 1, b, v] for b in range(local)]
                 pieces += [peer[k, x, b, v] for b in range(local)]
                 spectral = weighted(weights, pieces)
-                result[n][v] = rhs[n, v, x] - result[n][v] - speed * spectral
+                result[n][v] = cells[n, v, nvar, x] - result[n][v] - speed * spectral
         return result
 
     def far_side(k, x, n, v):
@@ -321,7 +324,7 @@
         for hop in hops:
             if k == 0:
                 pieces = [got[k, hop - 1, x, b, v] for b in range(local)]
-                pieces += [relayed[hop - 1, x, b, v] for b in range(local)]
+                pieces += [peer[ITERS + hop - 1, x, b, v] for b in range(local)]
                 term = weighted(weights_of(hop, n), pieces)
             else:
                 term = got[k, hop - 1, x, n, v]
@@ -351,14 +354,17 @@
             def _():
                 to_last(k).wait_recv()
 
-            both_sides(k, x).wait_recv()
+            @pl.when(step % group == 0)
+            def _():
+                both_sides(k, x).wait_recv()
+
             rights = near_side(k, x)
             if final_pass:
                 own = mine(k, x)
                 for n in range(local):
                     for v in range(nvar):
                         for w in range(nvar):
-                            rights[n][v] = rights[n][v] - blocks[n, v, w, x] * own[n][w]
+                            rights[n][v] = rights[n][v] - cells[n, v, w, x] * own[n][w]
             if k == 0:
 
                 @pl.when(step + 1 < planes)
@@ -402,7 +408,6 @@
         sent = got.at[:, hop - 1]
         remote(sent, sent, x_send.at[0], x_send.at[0], inst=partner).wait_send()
     remote(peer, peer, core_send.at[0], core_send.at[0], inst=partner).wait_send()
-    remote(relayed, relayed, core_send.at[1], core_send.at[1], inst=partner).wait_send()
     remote(edge_out, edge_out, edge_send.at[0], edge_send.at[0], inst=partner).wait_send()
     layer = cur.at[:, 0]
 
@@ -433,12 +438,14 @@
         local, nvar, planes, rows, depth = state.shape
         pairs = ranks // 2
         cell = (local, nvar, rows, depth)
+        group = GROUP if planes % GROUP == 0 else 1
         edge = pltpu.VMEM((ITERS, planes, 2, local * nvar, depth), jnp.float32)
         hbm = pl.BlockSpec(memory_space=pltpu.HBM)
         near = pl.BlockSpec(memory_space=pltpu.VMEM)
         dma = pltpu.SemaphoreType.DMA
         vmem = lambda *lead: pltpu.VMEM(lead + cell, jnp.float32)
         matrices = pltpu.VMEM(jacobian.shape, jnp.float32)
+        padded = (local, nvar, nvar + 1, planes, rows, depth)
         flows = couplings.transpose(1, 0, 2)
         field, residual = pl.pallas_call(
             functools.partial(kernel, ranks, count_x, count_y),
@@ -446,14 +453,13 @@
             in_specs=[hbm] * 5,
             out_specs=[near, near],
             scratch_shapes=[
-                vmem(ITERS, planes + 2), vmem(ITERS, planes),
+                vmem(ITERS, planes + 2), vmem(ITERS + pairs - 1, planes),
                 vmem(ITERS - 1, pairs - 1, planes), vmem(ITERS, pairs - 1, planes),
-                vmem(pairs - 1, planes), edge, edge,
-                pltpu.VMEM(state.shape, jnp.float32), matrices, matrices,
+                edge, edge, pltpu.VMEM(padded, jnp.float32), matrices,
                 pltpu.SMEM(flows.shape, jnp.float32), pltpu.SMEM(omega.shape, jnp.float32),
-                dma((5,)), dma((1,)), dma((2,)), dma((1,)), dma((2,)),
-                dma((1,)), dma((ITERS - 1, planes)), dma((pairs - 1, planes)),
-                dma((2, pairs - 1, planes)), dma((2, planes)), dma((2, ITERS)),
+                dma((4,)), dma((1,)), dma((1,)), dma((1,)), dma((2,)),
+                dma((1,)), dma((ITERS - 1 + max(pairs - 2, 0), planes)),
+                dma((2, pairs - 1, planes)), dma((2, planes // group)), dma((2, 2)),
                 pltpu.SemaphoreType.REGULAR((1,)),
             ],
             compiler_params=pltpu.CompilerParams(

time: 30 us -> 29.4 us (0.980)
  Pallas kernels: 28.6 us -> 28 us
    pallas_call x1, Pallas kernels: 27.7 us -> 27.1 us  [shards(): pl.pallas_call(functools.partial(kernel, ranks, count_x, count_y), out_sh...]
where the time goes in v2:
time: 29.4 us; the launch traced here: 29.3 us
  Pallas kernels  28 us (95%)
  between operations  1.29 us (4%)
    pallas_call x1, Pallas kernels, shards(): pl.pallas_call(functools.partial(kernel, ranks, count_x, count_y), out_sh...  27.1 us
    pallas_call x1, Pallas kernels, shards(): pl.pallas_call(store, out_shape=[jax.ShapeDtypeStruct(state.shape, jnp.fl...  0.85 us

profile of v2, /device:TPU:0, one launch (start us, length us, event | category | flops | bytes accessed | tf_op | source)
XLA Modules:
  0.0 29.3 jit_solution(15977761761142943006)
XLA Ops:
  1.3 27.1 %smooth.1 = (f32[2,5,8,8,128]{4,3,2,1,0:T(8,128)S(1)}, f32[2,5,8,8,128]{4,3,2,1,0:T(8,128)S(1)}) custom-call(f32[2,5,8,8,128]{4,3,2,1,0:T(8,128)} %state.1, f32[2,5,8,8,128]{4,3,2,1,0:T(8,128)} %source.1, f32[2,5,5,8,8,128]{5,4,3,2,1,0:T(8,128)} %jacobian.1, f32[5,6,5]{2,1,0:T(8,128)} %bitcast.1, f32[1]{0:T(128)S(6)} %copy.7.omega), custom_call_target="tpu_custom_call" | custom-call | tf_op jit(solution)/shard_map/smooth/pallas_call | solution.py:450
  28.4 0.9 %store.1 = (f32[2,5,8,8,128]{4,3,2,1,0:T(8,128)}, f32[2,5,8,8,128]{4,3,2,1,0:T(8,128)}) custom-call(f32[2,5,8,8,128]{4,3,2,1,0:T(8,128)S(1)} %get-tuple-element.4.field, f32[2,5,8,8,128]{4,3,2,1,0:T(8,128)S(1)} %get-tuple-element.5.residual), custom_call_target="tpu_custom_call" | custom-call | tf_op jit(solution)/shard_map/store/pallas_call | solution.py:469

commit v3 on v2

--- a/solution.py
+++ b/solution.py
@@ -139,6 +139,15 @@
             cur.at[k, 1], cur.at[k, planes + 1], side_send.at[1], side_recv.at[1, k % 2],
             gx=at_x - 1)
 
+    def send_layers(k):
+        @pl.when(has_high)
+        def _():
+            to_next(k).start()
+
+        @pl.when(has_low)
+        def _():
+            to_last(k).start()
+
     def send_planes(k, x):
         to_peer(k, x).start()
 
@@ -195,25 +204,24 @@
         pl.semaphore_signal(barrier, inc=1, device_id=where, device_id_type=MESH)
 
     leads = core == 1
-    lead = pair * 2 + 1
     tail = pair * 2
-
-    @pl.when(jnp.logical_not(leads))
-    def _():
-        greet(inst=lead)
-
-    for hop in hops:
-        greet(inst=((pair + hop) % pairs) * 2 + 1)
+    counts_inst = rank == ranks - 1
+    counts_side = rank == 1
+
+    @pl.when(jnp.logical_not(counts_inst))
+    def _():
+        greet(inst=ranks - 1)
+
     greet(inst=tail, gy=up)
     greet(inst=tail, gy=down)
 
     @pl.when(has_low)
     def _():
-        greet(inst=lead, gx=at_x - 1)
+        greet(inst=1, gx=at_x - 1)
 
     @pl.when(has_high)
     def _():
-        greet(inst=lead, gx=at_x + 1)
+        greet(inst=1, gx=at_x + 1)
 
     for step in range(planes):
         load_state(plane_of(step)).start()
@@ -234,36 +242,41 @@
 
     sides = has_low.astype(jnp.int32) + has_high.astype(jnp.int32)
     held = cur.at[0, 1:planes + 1]
+
+    def tell(stage, where):
+        pl.semaphore_signal(
+            ready.at[stage], inc=1, device_id={"inst": where}, device_id_type=MESH)
+
+    def gather(stage, counts, arrivals, others):
+        @pl.when(counts)
+        def _():
+            pl.semaphore_wait(barrier, arrivals)
+            for where in others:
+                tell(stage, where)
+
+        @pl.when(jnp.logical_not(counts))
+        def _():
+            pl.semaphore_wait(ready.at[stage], 1)
+
+    gather(0, counts_inst, ranks - 1, range(ranks - 1))
     pltpu.make_async_copy(held, held, load_sem.at[0]).wait()
-
-    def tell_partner():
-        pl.semaphore_signal(
-            ready.at[0], inc=1, device_id={"inst": partner}, device_id_type=MESH)
-
-    @pl.when(leads)
-    def _():
-        pl.semaphore_wait(barrier, 2 * pairs - 1 + 2 * sides)
-        tell_partner()
-
-    @pl.when(jnp.logical_not(leads))
-    def _():
-        pl.semaphore_wait(ready.at[0], 1)
 
     @pl.loop(0, planes)
     def _(step):
         x = plane_of(step)
         for hop in hops:
             to_pair(0, x, hop).start()
-        send_planes(0, x)
-
-    @pl.when(leads)
-    def _():
-        pl.semaphore_wait(ready.at[0], 1)
-
-    @pl.when(jnp.logical_not(leads))
-    def _():
-        pl.semaphore_wait(barrier, 4)
-        tell_partner()
+        to_peer(0, x).start()
+
+    def first_layers():
+        gather(1, counts_side, ranks * sides, [at for at in range(ranks) if at != 1])
+        send_layers(0)
+
+    @pl.when(at_y % 2 == 0)
+    def _():
+        first_layers()
+
+    gather(2, jnp.logical_not(leads), 4, [partner])
 
     @pl.loop(0, planes)
     def _(step):
@@ -271,6 +284,9 @@
         send_edges(0, x, mine(0, x))
         start_edges(0, x)
 
+    @pl.when(at_y % 2 == 1)
+    def _():
+        first_layers()
     pltpu.make_async_copy(cells, cells, load_sem.at[1]).wait()
     for copy in loads[2:]:
         copy.wait()
@@ -460,7 +476,7 @@
                 dma((4,)), dma((1,)), dma((1,)), dma((1,)), dma((2,)),
                 dma((1,)), dma((ITERS - 1 + max(pairs - 2, 0), planes)),
                 dma((2, pairs - 1, planes)), dma((2, planes // group)), dma((2, 2)),
-                pltpu.SemaphoreType.REGULAR((1,)),
+                pltpu.SemaphoreType.REGULAR((3,)),
             ],
             compiler_params=pltpu.CompilerParams(
                 collective_id=0, has_side_effects=True, vmem_limit_bytes=60 * 1024 * 1024),

time: 29.4 us -> 28.6 us (0.973)
  Pallas kernels: 28 us -> 27.1 us
    pallas_call x1, Pallas kernels: 27.1 us -> 26.3 us  [shards(): pl.pallas_call(functools.partial(kernel, ranks, count_x, count_y), out_sh...]
where the time goes in v3:
time: 28.6 us; the launch traced here: 28.4 us
  Pallas kernels  27.1 us (95%)
  between operations  1.29 us (5%)
    pallas_call x1, Pallas kernels, shards(): pl.pallas_call(functools.partial(kernel, ranks, count_x, count_y), out_sh...  26.3 us
    pallas_call x1, Pallas kernels, shards(): pl.pallas_call(store, out_shape=[jax.ShapeDtypeStruct(state.shape, jnp.fl...  0.85 us

profile of v3, /device:TPU:0, one launch (start us, length us, event | category | flops | bytes accessed | tf_op | source)
XLA Modules:
  0.0 28.4 jit_solution(10704605346957246534)
XLA Ops:
  1.3 26.3 %smooth.1 = (f32[2,5,8,8,128]{4,3,2,1,0:T(8,128)S(1)}, f32[2,5,8,8,128]{4,3,2,1,0:T(8,128)S(1)}) custom-call(f32[2,5,8,8,128]{4,3,2,1,0:T(8,128)} %state.1, f32[2,5,8,8,128]{4,3,2,1,0:T(8,128)} %source.1, f32[2,5,5,8,8,128]{5,4,3,2,1,0:T(8,128)} %jacobian.1, f32[5,6,5]{2,1,0:T(8,128)} %bitcast.1, f32[1]{0:T(128)S(6)} %copy.7.omega), custom_call_target="tpu_custom_call" | custom-call | tf_op jit(solution)/shard_map/smooth/pallas_call | solution.py:466
  27.6 0.9 %store.1 = (f32[2,5,8,8,128]{4,3,2,1,0:T(8,128)}, f32[2,5,8,8,128]{4,3,2,1,0:T(8,128)}) custom-call(f32[2,5,8,8,128]{4,3,2,1,0:T(8,128)S(1)} %get-tuple-element.4.field, f32[2,5,8,8,128]{4,3,2,1,0:T(8,128)S(1)} %get-tuple-element.5.residual), custom_call_target="tpu_custom_call" | custom-call | tf_op jit(solution)/shard_map/store/pallas_call | solution.py:485

commit v4 on v3

--- a/solution.py
+++ b/solution.py
@@ -305,7 +305,9 @@
     first_row, final_row = row_at == 0, row_at == rows - 1
     first_lane, final_lane = lane_at == 0, lane_at == depth - 1
     speed = speed_in[0]
-    lag = min(LAG, planes)
+    def lag_of(k):
+        return jnp.where(jnp.logical_and(leads, k == ITERS - 1), min(5, planes), min(LAG, planes))
+
 
     def near_side(k, x):
         result = [[None] * nvar for _ in range(local)]
@@ -410,15 +412,21 @@
                 send_planes(k + 1, x)
                 start_edges(k + 1, x)
 
-                @pl.when(step >= lag)
+                later = lag_of(k + 1)
+
+                @pl.when(step >= later)
                 def _():
-                    send_parts(k + 1, plane_of(step - lag))
+                    send_parts(k + 1, plane_of(step - later))
 
             if k > 0:
-
-                @pl.when(step < lag)
-                def _():
-                    send_parts(k, plane_of(planes - lag + step))
+                now = lag_of(k)
+
+                for j in range(2):
+                    at = step * 2 + j
+
+                    @pl.when(at < now)
+                    def _(at=at):
+                        send_parts(k, plane_of(planes - now + at))
 
     for hop in hops:
         sent = got.at[:, hop - 1]

time: 28.6 us -> 27.9 us (0.976)
  the two profiles are of different devices: /device:TPU:0 before, /device:TPU:1 now
where the time goes in v4:
time: 27.9 us; the launch traced here: 27.7 us
  Pallas kernels  26.5 us (95%)
  between operations  1.29 us (5%)
    pallas_call x1, Pallas kernels, shards(): pl.pallas_call(functools.partial(kernel, ranks, count_x, count_y), out_sh...  25.6 us
    pallas_call x1, Pallas kernels, shards(): pl.pallas_call(store, out_shape=[jax.ShapeDtypeStruct(state.shape, jnp.fl...  0.85 us

profile of v4, /device:TPU:1, one launch (start us, length us, event | category | flops | bytes accessed | tf_op | source)
XLA Modules:
  0.0 27.7 jit_solution(11013732994879811335)
XLA Ops:
  1.3 25.6 %smooth.1 = (f32[2,5,8,8,128]{4,3,2,1,0:T(8,128)S(1)}, f32[2,5,8,8,128]{4,3,2,1,0:T(8,128)S(1)}) custom-call(f32[2,5,8,8,128]{4,3,2,1,0:T(8,128)} %state.1, f32[2,5,8,8,128]{4,3,2,1,0:T(8,128)} %source.1, f32[2,5,5,8,8,128]{5,4,3,2,1,0:T(8,128)} %jacobian.1, f32[5,6,5]{2,1,0:T(8,128)} %bitcast.1, f32[1]{0:T(128)S(6)} %copy.7.omega), custom_call_target="tpu_custom_call" | custom-call | tf_op jit(solution)/shard_map/smooth/pallas_call | solution.py:474
  26.9 0.9 %store.1 = (f32[2,5,8,8,128]{4,3,2,1,0:T(8,128)}, f32[2,5,8,8,128]{4,3,2,1,0:T(8,128)}) custom-call(f32[2,5,8,8,128]{4,3,2,1,0:T(8,128)S(1)} %get-tuple-element.4.field, f32[2,5,8,8,128]{4,3,2,1,0:T(8,128)S(1)} %get-tuple-element.5.residual), custom_call_target="tpu_custom_call" | custom-call | tf_op jit(solution)/shard_map/store/pallas_call | solution.py:493

commit v5 on v4

--- a/solution.py
+++ b/solution.py
@@ -69,7 +69,7 @@
     cur, peer, part, got, edge_out, edge_in,
     cells, lu, weights_in, speed_in,
     load_sem, x_send, core_send, edge_send, side_send,
-    first_recv, peer_recv, got_recv, edge_recv, side_recv, ready,
+    first_recv, plane_recv, edge_recv, side_recv, ready,
 ):
     local, nvar, planes, rows, depth = state.shape
     total = local * ranks
@@ -91,8 +91,8 @@
     def plane_of(step):
         return jnp.where(flip, planes - 1 - step, step)
 
-    def load_state(x):
-        return pltpu.make_async_copy(state.at[:, :, x], cur.at[0, x + 1], load_sem.at[0])
+    def load_state(x, at):
+        return pltpu.make_async_copy(state.at[:, :, x], cur.at[0, x + 1], load_sem.at[at])
 
     loads = [
         pltpu.make_async_copy(jacobian, cells.at[:, :, :nvar], load_sem.at[1]),
@@ -106,20 +106,20 @@
             source_ref, target_ref, send, recv, device_id=where, device_id_type=MESH)
 
     def to_peer(k, x):
-        recv = first_recv.at[0] if k == 0 else peer_recv.at[k - 1, x]
+        recv = first_recv.at[0] if k == 0 else plane_recv.at[k - 1, x]
         return remote(cur.at[k, x + 1], peer.at[k, x], core_send.at[0], recv, inst=partner)
 
     def to_pair(k, x, hop):
         target = ((pair + hop) % pairs) * 2 + core
         outgoing = cur.at[0, x + 1] if k == 0 else part.at[k - 1, hop - 1, x]
         return remote(
-            outgoing, got.at[k, hop - 1, x], x_send.at[0], got_recv.at[k % 2, hop - 1, x],
-            inst=target)
+            outgoing, got.at[k, hop - 1, x], x_send.at[0],
+            plane_recv.at[3 * hop - 3 + 2 * (k % 2), x], inst=target)
 
     def relay(x, hop):
         return remote(
             got.at[0, hop - 1, x], peer.at[ITERS + hop - 1, x], core_send.at[0],
-            peer_recv.at[1 if hop == 1 else ITERS + hop - 3, x], inst=partner)
+            plane_recv.at[3 * hop - 2, x], inst=partner)
 
     def to_side(k, x, side):
         return remote(
@@ -198,6 +198,9 @@
                     part[k - 1, hop - 1, x, a, v] = weighted(weights, pieces)
             to_pair(k, x, hop).start()
 
+    for step in range(planes):
+        load_state(plane_of(step), 0 if step == 0 else 4).start()
+
     barrier = pltpu.get_barrier_semaphore()
 
     def greet(**where):
@@ -223,8 +226,6 @@
     def _():
         greet(inst=1, gx=at_x + 1)
 
-    for step in range(planes):
-        load_state(plane_of(step)).start()
     for copy in loads:
         copy.start()
 
@@ -241,7 +242,7 @@
             cur[k, planes + 1] = zero
 
     sides = has_low.astype(jnp.int32) + has_high.astype(jnp.int32)
-    held = cur.at[0, 1:planes + 1]
+    rest = cur.at[0, 1:planes]
 
     def tell(stage, where):
         pl.semaphore_signal(
@@ -259,14 +260,21 @@
             pl.semaphore_wait(ready.at[stage], 1)
 
     gather(0, counts_inst, ranks - 1, range(ranks - 1))
-    pltpu.make_async_copy(held, held, load_sem.at[0]).wait()
+    load_state(plane_of(0), 0).wait()
+
+    for hop in hops:
+        to_pair(0, plane_of(0), hop).start()
+
+    pltpu.make_async_copy(rest, rest, load_sem.at[4]).wait()
+
+    @pl.loop(1, planes)
+    def _(step):
+        for hop in hops:
+            to_pair(0, plane_of(step), hop).start()
 
     @pl.loop(0, planes)
     def _(step):
-        x = plane_of(step)
-        for hop in hops:
-            to_pair(0, x, hop).start()
-        to_peer(0, x).start()
+        to_peer(0, plane_of(step)).start()
 
     def first_layers():
         gather(1, counts_side, ranks * sides, [at for at in range(ranks) if at != 1])
@@ -481,9 +489,9 @@
                 vmem(ITERS - 1, pairs - 1, planes), vmem(ITERS, pairs - 1, planes),
                 edge, edge, pltpu.VMEM(padded, jnp.float32), matrices,
                 pltpu.SMEM(flows.shape, jnp.float32), pltpu.SMEM(omega.shape, jnp.float32),
-                dma((4,)), dma((1,)), dma((1,)), dma((1,)), dma((2,)),
-                dma((1,)), dma((ITERS - 1 + max(pairs - 2, 0), planes)),
-                dma((2, pairs - 1, planes)), dma((2, planes // group)), dma((2, 2)),
+                dma((5,)), dma((1,)), dma((1,)), dma((1,)), dma((2,)),
+                dma((1,)), dma((3 * (pairs - 1), planes)),
+                dma((2, planes // group)), dma((2, 2)),
                 pltpu.SemaphoreType.REGULAR((3,)),
             ],
             compiler_params=pltpu.CompilerParams(

time: 27.9 us -> 27.7 us (level)
  the two profiles are of different devices: /device:TPU:1 before, /device:TPU:0 now
where the time goes in v5:
time: 27.7 us; the launch traced here: 27.2 us
  Pallas kernels  25.9 us (94%)
  between operations  1.29 us (5%)
    pallas_call x1, Pallas kernels, shards(): pl.pallas_call(functools.partial(kernel, ranks, count_x, count_y), out_sh...  25.1 us
    pallas_call x1, Pallas kernels, shards(): pl.pallas_call(store, out_shape=[jax.ShapeDtypeStruct(state.shape, jnp.fl...  0.85 us

profile of v5, /device:TPU:0, one launch (start us, length us, event | category | flops | bytes accessed | tf_op | source)
XLA Modules:
  0.0 27.2 jit_solution(6370755690669952532)
XLA Ops:
  1.3 25.1 %smooth.1 = (f32[2,5,8,8,128]{4,3,2,1,0:T(8,128)S(1)}, f32[2,5,8,8,128]{4,3,2,1,0:T(8,128)S(1)}) custom-call(f32[2,5,8,8,128]{4,3,2,1,0:T(8,128)} %state.1, f32[2,5,8,8,128]{4,3,2,1,0:T(8,128)} %source.1, f32[2,5,5,8,8,128]{5,4,3,2,1,0:T(8,128)} %jacobian.1, f32[5,6,5]{2,1,0:T(8,128)} %bitcast.1, f32[1]{0:T(128)S(6)} %copy.7.omega), custom_call_target="tpu_custom_call" | custom-call | tf_op jit(solution)/shard_map/smooth/pallas_call | solution.py:482
  26.4 0.9 %store.1 = (f32[2,5,8,8,128]{4,3,2,1,0:T(8,128)}, f32[2,5,8,8,128]{4,3,2,1,0:T(8,128)}) custom-call(f32[2,5,8,8,128]{4,3,2,1,0:T(8,128)S(1)} %get-tuple-element.4.field, f32[2,5,8,8,128]{4,3,2,1,0:T(8,128)S(1)} %get-tuple-element.5.residual), custom_call_target="tpu_custom_call" | custom-call | tf_op jit(solution)/shard_map/store/pallas_call | solution.py:501

commit v6 on v5

--- a/solution.py
+++ b/solution.py
@@ -198,9 +198,6 @@
                     part[k - 1, hop - 1, x, a, v] = weighted(weights, pieces)
             to_pair(k, x, hop).start()
 
-    for step in range(planes):
-        load_state(plane_of(step), 0 if step == 0 else 4).start()
-
     barrier = pltpu.get_barrier_semaphore()
 
     def greet(**where):
@@ -215,6 +212,9 @@
     def _():
         greet(inst=ranks - 1)
 
+    for step in range(planes):
+        load_state(plane_of(step), 0 if step == 0 else 4).start()
+
     greet(inst=tail, gy=up)
     greet(inst=tail, gy=down)
 
@@ -225,21 +225,6 @@
     @pl.when(has_high)
     def _():
         greet(inst=1, gx=at_x + 1)
-
-    for copy in loads:
-        copy.start()
-
-    zero = jnp.zeros((local, nvar, rows, depth), jnp.float32)
-
-    @pl.when(jnp.logical_not(has_low))
-    def _():
-        for k in range(ITERS):
-            cur[k, 0] = zero
-
-    @pl.when(jnp.logical_not(has_high))
-    def _():
-        for k in range(ITERS):
-            cur[k, planes + 1] = zero
 
     sides = has_low.astype(jnp.int32) + has_high.astype(jnp.int32)
     rest = cur.at[0, 1:planes]
@@ -272,9 +257,24 @@
         for hop in hops:
             to_pair(0, plane_of(step), hop).start()
 
+    for copy in loads:
+        copy.start()
+
     @pl.loop(0, planes)
     def _(step):
         to_peer(0, plane_of(step)).start()
+
+    zero = jnp.zeros((local, nvar, rows, depth), jnp.float32)
+
+    @pl.when(jnp.logical_not(has_low))
+    def _():
+        for k in range(ITERS):
+            cur[k, 0] = zero
+
+    @pl.when(jnp.logical_not(has_high))
+    def _():
+        for k in range(ITERS):
+            cur[k, planes + 1] = zero
 
     def first_layers():
         gather(1, counts_side, ranks * sides, [at for at in range(ranks) if at != 1])

time: 27.7 us -> 27.7 us (level)
  no operation moved by 1% of the time
where the time goes in v6:
time: 27.7 us; the launch traced here: 27.2 us
  Pallas kernels  25.9 us (94%)
  between operations  1.29 us (5%)
    pallas_call x1, Pallas kernels, shards(): pl.pallas_call(functools.partial(kernel, ranks, count_x, count_y), out_sh...  25 us
    pallas_call x1, Pallas kernels, shards(): pl.pallas_call(store, out_shape=[jax.ShapeDtypeStruct(state.shape, jnp.fl...  0.85 us

profile of v6, /device:TPU:0, one launch (start us, length us, event | category | flops | bytes accessed | tf_op | source)
XLA Modules:
  0.0 27.2 jit_solution(11313999845639469117)
XLA Ops:
  1.3 25.0 %smooth.1 = (f32[2,5,8,8,128]{4,3,2,1,0:T(8,128)S(1)}, f32[2,5,8,8,128]{4,3,2,1,0:T(8,128)S(1)}) custom-call(f32[2,5,8,8,128]{4,3,2,1,0:T(8,128)} %state.1, f32[2,5,8,8,128]{4,3,2,1,0:T(8,128)} %source.1, f32[2,5,5,8,8,128]{5,4,3,2,1,0:T(8,128)} %jacobian.1, f32[5,6,5]{2,1,0:T(8,128)} %bitcast.1, f32[1]{0:T(128)S(6)} %copy.7.omega), custom_call_target="tpu_custom_call" | custom-call | tf_op jit(solution)/shard_map/smooth/pallas_call | solution.py:482
  26.3 0.9 %store.1 = (f32[2,5,8,8,128]{4,3,2,1,0:T(8,128)}, f32[2,5,8,8,128]{4,3,2,1,0:T(8,128)}) custom-call(f32[2,5,8,8,128]{4,3,2,1,0:T(8,128)S(1)} %get-tuple-element.4.field, f32[2,5,8,8,128]{4,3,2,1,0:T(8,128)S(1)} %get-tuple-element.5.residual), custom_call_target="tpu_custom_call" | custom-call | tf_op jit(solution)/shard_map/store/pallas_call | solution.py:501

commit v7 on v6

--- a/solution.py
+++ b/solution.py
@@ -69,7 +69,7 @@
     cur, peer, part, got, edge_out, edge_in,
     cells, lu, weights_in, speed_in,
     load_sem, x_send, core_send, edge_send, side_send,
-    first_recv, plane_recv, edge_recv, side_recv, ready,
+    first_recv, plane_recv, pair_recv, edge_recv, side_recv, ready,
 ):
     local, nvar, planes, rows, depth = state.shape
     total = local * ranks
@@ -92,13 +92,13 @@
         return jnp.where(flip, planes - 1 - step, step)
 
     def load_state(x, at):
-        return pltpu.make_async_copy(state.at[:, :, x], cur.at[0, x + 1], load_sem.at[at])
+        return pltpu.make_async_copy(state.at[:, :, x], cur.at[0, x + 1], edge_recv.at[1, at])
 
     loads = [
-        pltpu.make_async_copy(jacobian, cells.at[:, :, :nvar], load_sem.at[1]),
-        pltpu.make_async_copy(source, cells.at[:, :, nvar], load_sem.at[1]),
-        pltpu.make_async_copy(couplings, weights_in, load_sem.at[2]),
-        pltpu.make_async_copy(omega, speed_in, load_sem.at[3]),
+        pltpu.make_async_copy(jacobian, cells.at[:, :, :nvar], load_sem.at[0]),
+        pltpu.make_async_copy(source, cells.at[:, :, nvar], load_sem.at[0]),
+        pltpu.make_async_copy(couplings, weights_in, load_sem.at[1]),
+        pltpu.make_async_copy(omega, speed_in, load_sem.at[2]),
     ]
 
     def remote(source_ref, target_ref, send, recv, **where):
@@ -108,18 +108,23 @@
     def to_peer(k, x):
         recv = first_recv.at[0] if k == 0 else plane_recv.at[k - 1, x]
         return remote(cur.at[k, x + 1], peer.at[k, x], core_send.at[0], recv, inst=partner)
+
+    def got_recv(k, x, hop):
+        if k % 2 == 1:
+            return pair_recv.at[hop - 1, x // group]
+        return plane_recv.at[2 * hop - 2, x]
 
     def to_pair(k, x, hop):
         target = ((pair + hop) % pairs) * 2 + core
         outgoing = cur.at[0, x + 1] if k == 0 else part.at[k - 1, hop - 1, x]
         return remote(
             outgoing, got.at[k, hop - 1, x], x_send.at[0],
-            plane_recv.at[3 * hop - 3 + 2 * (k % 2), x], inst=target)
+            got_recv(k, x, hop), inst=target)
 
     def relay(x, hop):
         return remote(
             got.at[0, hop - 1, x], peer.at[ITERS + hop - 1, x], core_send.at[0],
-            plane_recv.at[3 * hop - 2, x], inst=partner)
+            plane_recv.at[2 * hop - 1, x], inst=partner)
 
     def to_side(k, x, side):
         return remote(
@@ -213,7 +218,7 @@
         greet(inst=ranks - 1)
 
     for step in range(planes):
-        load_state(plane_of(step), 0 if step == 0 else 4).start()
+        load_state(plane_of(step), min(step, 1)).start()
 
     greet(inst=tail, gy=up)
     greet(inst=tail, gy=down)
@@ -250,7 +255,7 @@
     for hop in hops:
         to_pair(0, plane_of(0), hop).start()
 
-    pltpu.make_async_copy(rest, rest, load_sem.at[4]).wait()
+    pltpu.make_async_copy(rest, rest, edge_recv.at[1, 1]).wait()
 
     @pl.loop(1, planes)
     def _(step):
@@ -295,7 +300,7 @@
     @pl.when(at_y % 2 == 1)
     def _():
         first_layers()
-    pltpu.make_async_copy(cells, cells, load_sem.at[1]).wait()
+    pltpu.make_async_copy(cells, cells, load_sem.at[0]).wait()
     for copy in loads[2:]:
         copy.wait()
 
@@ -401,7 +406,16 @@
                     relay(x, hop).wait_recv()
             else:
                 for hop in hops:
-                    to_pair(k, x, hop).wait_recv()
+                    if k % 2 == 0:
+                        to_pair(k, x, hop).wait_recv()
+                        continue
+
+                    @pl.when(step % group == 0)
+                    def _(hop=hop):
+                        both = got.at[k, hop - 1, :group]
+                        remote(
+                            both, both, x_send.at[0], got_recv(k, x, hop),
+                            inst=partner).wait_recv()
             fields = []
             for n in range(local):
                 right = rights[n]
@@ -489,9 +503,9 @@
                 vmem(ITERS - 1, pairs - 1, planes), vmem(ITERS, pairs - 1, planes),
                 edge, edge, pltpu.VMEM(padded, jnp.float32), matrices,
                 pltpu.SMEM(flows.shape, jnp.float32), pltpu.SMEM(omega.shape, jnp.float32),
-                dma((5,)), dma((1,)), dma((1,)), dma((1,)), dma((2,)),
-                dma((1,)), dma((3 * (pairs - 1), planes)),
-                dma((2, planes // group)), dma((2, 2)),
+                dma((3,)), dma((1,)), dma((1,)), dma((1,)), dma((2,)),
+                dma((1,)), dma((2 * (pairs - 1), planes)), dma((pairs - 1, planes // group)),
+                dma((2, max(planes // group, 2))), dma((2, 2)),
                 pltpu.SemaphoreType.REGULAR((3,)),
             ],
             compiler_params=pltpu.CompilerParams(

time: 27.7 us -> 27.8 us (level)
  no operation moved by 1% of the time
where the time goes in v7:
time: 27.8 us; the launch traced here: 27.4 us
  Pallas kernels  26.1 us (94%)
  between operations  1.29 us (5%)
    pallas_call x1, Pallas kernels, shards(): pl.pallas_call(functools.partial(kernel, ranks, count_x, count_y), out_sh...  25.2 us
    pallas_call x1, Pallas kernels, shards(): pl.pallas_call(store, out_shape=[jax.ShapeDtypeStruct(state.shape, jnp.fl...  0.85 us

profile of v7, /device:TPU:0, one launch (start us, length us, event | category | flops | bytes accessed | tf_op | source)
XLA Modules:
  0.0 27.4 jit_solution(10318661727949100481)
XLA Ops:
  1.3 25.2 %smooth.1 = (f32[2,5,8,8,128]{4,3,2,1,0:T(8,128)S(1)}, f32[2,5,8,8,128]{4,3,2,1,0:T(8,128)S(1)}) custom-call(f32[2,5,8,8,128]{4,3,2,1,0:T(8,128)} %state.1, f32[2,5,8,8,128]{4,3,2,1,0:T(8,128)} %source.1, f32[2,5,5,8,8,128]{5,4,3,2,1,0:T(8,128)} %jacobian.1, f32[5,6,5]{2,1,0:T(8,128)} %bitcast.1, f32[1]{0:T(128)S(6)} %copy.7.omega), custom_call_target="tpu_custom_call" | custom-call | tf_op jit(solution)/shard_map/smooth/pallas_call | solution.py:496
  26.5 0.9 %store.1 = (f32[2,5,8,8,128]{4,3,2,1,0:T(8,128)}, f32[2,5,8,8,128]{4,3,2,1,0:T(8,128)}) custom-call(f32[2,5,8,8,128]{4,3,2,1,0:T(8,128)S(1)} %get-tuple-element.4.field, f32[2,5,8,8,128]{4,3,2,1,0:T(8,128)S(1)} %get-tuple-element.5.residual), custom_call_target="tpu_custom_call" | custom-call | tf_op jit(solution)/shard_map/store/pallas_call | solution.py:515

commit v8 on v5

--- a/solution.py
+++ b/solution.py
@@ -227,7 +227,7 @@
         greet(inst=1, gx=at_x + 1)
 
     for copy in loads:
-        copy.start()
+        copy.start(priority=1)
 
     zero = jnp.zeros((local, nvar, rows, depth), jnp.float32)
 
@@ -457,8 +457,8 @@
         pltpu.make_async_copy(field, state_next, sems.at[0]),
         pltpu.make_async_copy(residual, last_residual, sems.at[1]),
     ]
-    for copy in copies:
-        copy.start()
+    for queue, copy in enumerate(copies):
+        copy.start(priority=queue)
     for copy in copies:
         copy.wait()
 

time: 27.7 us -> 27.7 us (level)
  no operation moved by 1% of the time
where the time goes in v8:
time: 27.7 us; the launch traced here: 27.2 us
  Pallas kernels  25.9 us (94%)
  between operations  1.29 us (5%)
    pallas_call x1, Pallas kernels, shards(): pl.pallas_call(functools.partial(kernel, ranks, count_x, count_y), out_sh...  25.1 us
    pallas_call x1, Pallas kernels, shards(): pl.pallas_call(store, out_shape=[jax.ShapeDtypeStruct(state.shape, jnp.fl...  0.85 us

profile of v8, /device:TPU:0, one launch (start us, length us, event | category | flops | bytes accessed | tf_op | source)
XLA Modules:
  0.0 27.2 jit_solution(3303840475098495842)
XLA Ops:
  1.3 25.1 %smooth.1 = (f32[2,5,8,8,128]{4,3,2,1,0:T(8,128)S(1)}, f32[2,5,8,8,128]{4,3,2,1,0:T(8,128)S(1)}) custom-call(f32[2,5,8,8,128]{4,3,2,1,0:T(8,128)} %state.1, f32[2,5,8,8,128]{4,3,2,1,0:T(8,128)} %source.1, f32[2,5,5,8,8,128]{5,4,3,2,1,0:T(8,128)} %jacobian.1, f32[5,6,5]{2,1,0:T(8,128)} %bitcast.1, f32[1]{0:T(128)S(6)} %copy.7.omega), custom_call_target="tpu_custom_call" | custom-call | tf_op jit(solution)/shard_map/smooth/pallas_call | solution.py:482
  26.4 0.9 %store.1 = (f32[2,5,8,8,128]{4,3,2,1,0:T(8,128)}, f32[2,5,8,8,128]{4,3,2,1,0:T(8,128)}) custom-call(f32[2,5,8,8,128]{4,3,2,1,0:T(8,128)S(1)} %get-tuple-element.4.field, f32[2,5,8,8,128]{4,3,2,1,0:T(8,128)S(1)} %get-tuple-element.5.residual), custom_call_target="tpu_custom_call" | custom-call | tf_op jit(solution)/shard_map/store/pallas_call | solution.py:501

commit v9 on v5

--- a/solution.py
+++ b/solution.py
@@ -314,7 +314,7 @@
     first_lane, final_lane = lane_at == 0, lane_at == depth - 1
     speed = speed_in[0]
     def lag_of(k):
-        return jnp.where(jnp.logical_and(leads, k == ITERS - 1), min(5, planes), min(LAG, planes))
+        return jnp.where(jnp.logical_and(leads, k == ITERS - 1), min(6, planes), min(LAG, planes))
 
 
     def near_side(k, x):
@@ -429,8 +429,8 @@
             if k > 0:
                 now = lag_of(k)
 
-                for j in range(2):
-                    at = step * 2 + j
+                for j in range(6):
+                    at = step * 6 + j
 
                     @pl.when(at < now)
                     def _(at=at):

time: 27.7 us -> 27.9 us (level)
  the two profiles are of different devices: /device:TPU:0 before, /device:TPU:1 now
where the time goes in v9:
time: 27.9 us; the launch traced here: 27.7 us
  Pallas kernels  26.5 us (95%)
  between operations  1.29 us (5%)
    pallas_call x1, Pallas kernels, shards(): pl.pallas_call(functools.partial(kernel, ranks, count_x, count_y), out_sh...  25.6 us
    pallas_call x1, Pallas kernels, shards(): pl.pallas_call(store, out_shape=[jax.ShapeDtypeStruct(state.shape, jnp.fl...  0.85 us

profile of v9, /device:TPU:1, one launch (start us, length us, event | category | flops | bytes accessed | tf_op | source)
XLA Modules:
  0.0 27.7 jit_solution(11122749755969717668)
XLA Ops:
  1.3 25.6 %smooth.1 = (f32[2,5,8,8,128]{4,3,2,1,0:T(8,128)S(1)}, f32[2,5,8,8,128]{4,3,2,1,0:T(8,128)S(1)}) custom-call(f32[2,5,8,8,128]{4,3,2,1,0:T(8,128)} %state.1, f32[2,5,8,8,128]{4,3,2,1,0:T(8,128)} %source.1, f32[2,5,5,8,8,128]{5,4,3,2,1,0:T(8,128)} %jacobian.1, f32[5,6,5]{2,1,0:T(8,128)} %bitcast.1, f32[1]{0:T(128)S(6)} %copy.7.omega), custom_call_target="tpu_custom_call" | custom-call | tf_op jit(solution)/shard_map/smooth/pallas_call | solution.py:482
  26.9 0.9 %store.1 = (f32[2,5,8,8,128]{4,3,2,1,0:T(8,128)}, f32[2,5,8,8,128]{4,3,2,1,0:T(8,128)}) custom-call(f32[2,5,8,8,128]{4,3,2,1,0:T(8,128)S(1)} %get-tuple-element.4.field, f32[2,5,8,8,128]{4,3,2,1,0:T(8,128)S(1)} %get-tuple-element.5.residual), custom_call_target="tpu_custom_call" | custom-call | tf_op jit(solution)/shard_map/store/pallas_call | solution.py:501

commit v10 on v6

--- a/solution.py
+++ b/solution.py
@@ -244,7 +244,7 @@
         def _():
             pl.semaphore_wait(ready.at[stage], 1)
 
-    gather(0, counts_inst, ranks - 1, range(ranks - 1))
+    gather(0, counts_inst, ranks - 1, range(ranks - 2, -1, -1))
     load_state(plane_of(0), 0).wait()
 
     for hop in hops:
@@ -258,7 +258,7 @@
             to_pair(0, plane_of(step), hop).start()
 
     for copy in loads:
-        copy.start()
+        copy.start(priority=1)
 
     @pl.loop(0, planes)
     def _(step):

time: 27.7 us -> 27.7 us (level)
  no operation moved by 1% of the time
where the time goes in v10:
time: 27.7 us; the launch traced here: 27.2 us
  Pallas kernels  25.9 us (94%)
  between operations  1.29 us (5%)
    pallas_call x1, Pallas kernels, shards(): pl.pallas_call(functools.partial(kernel, ranks, count_x, count_y), out_sh...  25 us
    pallas_call x1, Pallas kernels, shards(): pl.pallas_call(store, out_shape=[jax.ShapeDtypeStruct(state.shape, jnp.fl...  0.85 us

profile of v10, /device:TPU:0, one launch (start us, length us, event | category | flops | bytes accessed | tf_op | source)
XLA Modules:
  0.0 27.2 jit_solution(16127091114822033047)
XLA Ops:
  1.3 25.0 %smooth.1 = (f32[2,5,8,8,128]{4,3,2,1,0:T(8,128)S(1)}, f32[2,5,8,8,128]{4,3,2,1,0:T(8,128)S(1)}) custom-call(f32[2,5,8,8,128]{4,3,2,1,0:T(8,128)} %state.1, f32[2,5,8,8,128]{4,3,2,1,0:T(8,128)} %source.1, f32[2,5,5,8,8,128]{5,4,3,2,1,0:T(8,128)} %jacobian.1, f32[5,6,5]{2,1,0:T(8,128)} %bitcast.1, f32[1]{0:T(128)S(6)} %copy.7.omega), custom_call_target="tpu_custom_call" | custom-call | tf_op jit(solution)/shard_map/smooth/pallas_call | solution.py:482
  26.3 0.9 %store.1 = (f32[2,5,8,8,128]{4,3,2,1,0:T(8,128)}, f32[2,5,8,8,128]{4,3,2,1,0:T(8,128)}) custom-call(f32[2,5,8,8,128]{4,3,2,1,0:T(8,128)S(1)} %get-tuple-element.4.field, f32[2,5,8,8,128]{4,3,2,1,0:T(8,128)S(1)} %get-tuple-element.5.residual), custom_call_target="tpu_custom_call" | custom-call | tf_op jit(solution)/shard_map/store/pallas_call | solution.py:501
